TPU v7x, 128 devices: a whole 4x4x4 slice. The times are simulated.
128 devices in a mesh: dp: 16 (over x, z_hi, core), fsdp: 8 (over z_lo, y).
Axes of the slice: x: 4, y: 4, z: 4 (z_hi: 2, z_lo: 2; z = z_hi * 2 + z_lo), core: 2. Of those that a mesh axis runs over, the one named last changes fastest.
Arguments:
- activations: bfloat16 [98304, 8192], P(('dp', 'fsdp')), may hold values from -6 to 6
- out_grad: bfloat16 [98304, 1024], P(('dp', 'fsdp')), may hold values from -24 to 24
- master: float32 [1024, 8192], P('fsdp', 'dp'), may hold values from -0.0625 to 0.0625
- moment1: float32 [1024, 8192], P('fsdp', 'dp'), may hold values from -6 to 6
- moment2: float32 [1024, 8192], P('fsdp', 'dp'), may hold values from 0.2 to 5
Outputs:
- new_weight: bfloat16 [1024, 8192], P('fsdp')
- master_out: float32 [1024, 8192], P('fsdp', 'dp')
- moment1_out: float32 [1024, 8192], P('fsdp', 'dp')
- moment2_out: float32 [1024, 8192], P('fsdp', 'dp')
All inputs are finite; a program needn't handle non-finite values.
Results may differ from a plain program's by a relative error of at most 0.005.
Values may be sent and summed in bfloat16 or wider, within the bound.
No kernel may reach another device: no remote copies, remote signals or barrier semaphores. Data moves between devices by JAX's collectives and lax.ppermute only.
A program may use at most 128 MiB of HBM per device.

v0:
```python
import functools
import itertools

import jax
import jax.numpy as jnp
from jax import lax
from jax.experimental import pallas as pl
from jax.experimental.pallas import tpu as pltpu
from jax.sharding import PartitionSpec as P


STEP = 3
AXES = ("dp", "fsdp")


def place(x, z, c, y):
    x, z, y = x % 4, z % 4, y % 4
    return ((x * 2 + z // 2) * 2 + c) * 8 + (z % 2) * 4 + y


def moved(step):
    pairs = []
    for x, z, c, y in itertools.product(range(4), range(4), range(2), range(4)):
        dx, dz, dc, dy = step(c)
        pairs.append((place(x, z, c, y), place(x + dx, z + dz, c ^ dc, y + dy)))
    return pairs


def send(value, step):
    return lax.ppermute(value, AXES, moved(step))


def swap_cores(value):
    return send(value, lambda c: (0, 0, 1, 0))


def along_first(d):
    return lambda c: (d, 0, 0, 0) if c == 0 else (0, 0, 0, d)


def along_second(d):
    return lambda c: (0, 0, 0, d) if c == 0 else (d, 0, 0, 0)


def along_z(d):
    return lambda c: (0, d, 0, 0)


def product_kernel(scale, place_ref, grad_ref, first_ref, second_ref, far_ref, rest_ref, buf, sems):
    step = pl.program_id(0)
    slot = step % 2
    first = place_ref[0] == 0

    def each(step, slot, act):
        for y in range(4):
            one, other = jnp.where(first, step, y), jnp.where(first, y, step)
            hops = (one - place_ref[1]) & 3

            @pl.when(hops == 2)
            def _():
                act(pltpu.make_async_copy(buf.at[slot, y], far_ref.at[other], sems.at[slot, y]))

            @pl.when(hops != 2)
            def _():
                target = rest_ref.at[jnp.where(hops == 0, 2, hops >> 1), other]
                act(pltpu.make_async_copy(buf.at[slot, y], target, sems.at[slot, y]))

    @pl.when(step >= 2)
    def _():
        each(step - 2, slot, lambda copy: copy.wait())

    for i, act_ref in enumerate((first_ref, second_ref)):
        value = lax.dot_general(
            grad_ref[...], act_ref[...], (((0,), (0,)), ((), ())), preferred_element_type=jnp.float32
        )
        value = (value * scale).astype(jnp.bfloat16).reshape(2, 4, 128, 512)
        for low in range(2):
            for y in range(4):
                buf[slot, y, 2 * i + low] = value[low, y]
    each(step, slot, lambda copy: copy.start())

    @pl.when(step == 3)
    def _():
        each(step - 1, 1 - slot, lambda copy: copy.wait())
        each(step, slot, lambda copy: copy.wait())


def products(place, out_grad, act, scale):
    tokens = act.shape[0]
    shapes = [(4, 4, 128, 512), (3, 4, 4, 128, 512)]
    return pl.pallas_call(
        functools.partial(product_kernel, scale),
        grid_spec=pltpu.PrefetchScalarGridSpec(
            num_scalar_prefetch=1,
            grid=(4,),
            in_specs=[
                pl.BlockSpec((tokens, 1024), lambda k, h: (0, 0)),
                pl.BlockSpec((tokens, 512), lambda k, h: (0, 4 * k + h[0])),
                pl.BlockSpec((tokens, 512), lambda k, h: (0, 4 * k + 2 + h[0])),
            ],
            out_specs=[pl.BlockSpec(memory_space=pl.ANY)] * 2,
            scratch_shapes=[
                pltpu.VMEM((2, 4, 4, 128, 512), jnp.bfloat16),
                pltpu.SemaphoreType.DMA((2, 4)),
            ],
        ),
        out_shape=[jax.ShapeDtypeStruct(s, jnp.bfloat16) for s in shapes],
        compiler_params=pltpu.CompilerParams(dimension_semantics=("arbitrary",)),
        cost_estimate=pl.CostEstimate(
            flops=2 * 1024 * tokens * 4096, bytes_accessed=tokens * 8192, transcendentals=0
        ),
    )(place, out_grad, act, act)


def fold_kernel(two_ref, keep_ref, *refs):
    low_refs, high_refs, out_refs = refs[:2], refs[2:4], refs[4:]
    pieces = ((2, 0, 2), (2, 2, 2), (1, 0, 2), (3, 2, 2), (1, 2, 2), (3, 0, 2), (0, 0, 4))
    for (hops, start, count), out_ref in zip(pieces, out_refs):
        turn = (two_ref[0] + hops) & 3

        def write(refs, local, out_ref=out_ref, start=start, count=count, turn=turn):
            def rows(n, carry):
                i, row = n // 4, pl.multiple_of(n % 4 * 32, 32)
                cut = pl.ds(row, 32)
                values = [keep_ref[turn, start + i, cut]] + [r[local, start + i, cut] for r in refs]
                out_ref[i, cut] = total(values).astype(jnp.bfloat16)
                return carry

            lax.fori_loop(0, 4 * count, rows, 0)

        @pl.when(turn < 2)
        def _():
            write(low_refs, turn)

        @pl.when(turn >= 2)
        def _():
            write(high_refs, turn - 2)


def fold(two, keep, low, high):
    counts = (2, 2, 2, 2, 2, 2, 4)
    return pl.pallas_call(
        fold_kernel,
        in_specs=[pl.BlockSpec(memory_space=pltpu.SMEM)]
        + [pl.BlockSpec(memory_space=pltpu.VMEM)] * 5,
        out_specs=[pl.BlockSpec(memory_space=pltpu.VMEM)] * 7,
        out_shape=[jax.ShapeDtypeStruct((n, 128, 512), jnp.bfloat16) for n in counts],
        compiler_params=pltpu.CompilerParams(vmem_limit_bytes=16 * 2**20),
        cost_estimate=pl.CostEstimate(flops=2**24, bytes_accessed=2**23, transcendentals=0),
    )(two, keep, *low, *high)


def assemble_kernel(dp_ref, *refs):
    ins, out_ref, sems = refs[:9], refs[9], refs[10]
    dp = dp_ref[0]
    x, zh, c = dp >> 2, (dp >> 1) & 1, dp & 1
    copies = []

    def place(piece, x, zh, c):
        start = pl.multiple_of(((x & 3) * 4 + zh * 2 + c) * 512, 512)
        n = len(copies)
        copies.append(pltpu.make_async_copy(piece, out_ref.at[:, pl.ds(start, 512)], sems.at[n]))

    for i in range(2):
        place(ins[0].at[i], x, zh, c ^ i)
        for owner, held in ((c, ins[1:5]), (1 - c, ins[5:9])):
            side = x + 3 + 2 * owner
            place(held[0].at[i], side, zh, owner ^ i)
            place(held[1].at[i], side, 1 - zh, owner ^ i)
            place(held[2].at[i], x + 2, zh ^ owner, owner ^ i)
            if i == 0:
                place(held[3], x, 1 - zh, owner)
    for copy in copies:
        copy.start()
    for copy in copies:
        copy.wait()


def assemble(dp, *pieces):
    return pl.pallas_call(
        assemble_kernel,
        in_specs=[pl.BlockSpec(memory_space=pltpu.SMEM)]
        + [pl.BlockSpec(memory_space=pltpu.VMEM)] * 9,
        out_specs=pl.BlockSpec(memory_space=pl.ANY),
        out_shape=jax.ShapeDtypeStruct((128, 8192), jnp.bfloat16),
        scratch_shapes=[pltpu.SemaphoreType.DMA((16,))],
        compiler_params=pltpu.CompilerParams(vmem_limit_bytes=8 * 2**20),
    )(dp, *pieces)


def gathered(dp, weight):
    over = send(weight, lambda c: (0, 2, 0, 0))
    both = jnp.stack([weight, swap_cores(weight)])
    held = [
        send(both, lambda c: (1 - 2 * c, 0, 0, 0)),
        send(both, lambda c: (1 - 2 * c, 2, 0, 0)),
        send(both, lambda c: (2, 2 * c, 0, 0)),
        over,
    ]
    return assemble(dp, both, *held, *(swap_cores(v) for v in held))


def at(value, index, dim):
    return lax.dynamic_index_in_dim(value, index, dim, keepdims=False)


def scalars(*values):
    return jnp.stack(values).astype(jnp.int32)


def total(pieces):
    return functools.reduce(lambda a, b: a + b, [p.astype(jnp.float32) for p in pieces])


def step_of(activations, out_grad, master, moment1, moment2):
    scale = float(activations.shape[0] * 128) ** (-0.5)
    dp, fsdp = lax.axis_index("dp"), lax.axis_index("fsdp")
    x, zh, c = dp // 4, dp // 2 % 2, dp % 2
    zl, y = fsdp // 4, fsdp % 4
    z = zh * 2 + zl
    first = c == 0
    one, two = jnp.where(first, x, y), jnp.where(first, y, x)


    def added(*values):
        return total(values).astype(jnp.bfloat16)

    sent_far, sent_rest = products(scalars(1 - c, two), out_grad, activations, scale)
    got_far, got_rest = swap_cores(sent_far), swap_cores(sent_rest)
    own_far, own_rest = products(scalars(c, one), out_grad, activations, scale)

    far_low, far_high = added(own_far[:2], got_far[:2]), added(own_far[2:], got_far[2:])
    low, high = send(far_low, along_first(3)), send(far_high, along_first(1))
    (own_rest, got_rest), _ = lax.optimization_barrier(((own_rest, got_rest), (far_low, far_high)))
    up_low = added(own_rest[0, :2], got_rest[0, :2])
    down_high = added(own_rest[1, 2:], got_rest[1, 2:])
    (own_rest, got_rest), _ = lax.optimization_barrier(((own_rest, got_rest), (up_low, down_high)))
    up_high = added(own_rest[0, 2:], got_rest[0, 2:], high)
    down_low = added(own_rest[1, :2], got_rest[1, :2], low)
    keep = lax.optimization_barrier(added(own_rest[2], got_rest[2]))
    up_low, down_high = send(up_low, along_first(1)), send(down_high, along_first(3))
    lows = up_low, send(down_low, along_first(3))
    highs = send(up_high, along_first(1)), down_high
    far_low, far_high, up_low, down_high, up_high, down_low, keep = fold(scalars(two), keep, lows, highs)

    decayed1, decayed2 = lax.optimization_barrier((0.9 * moment1, 0.95 * moment2))
    low, high = send(far_low, along_second(3)), send(far_high, along_second(1))
    up_low, down_high = send(up_low, along_second(1)), send(down_high, along_second(3))
    up_high = send(added(up_high, high), along_second(1))
    down_low = send(added(down_low, low), along_second(3))
    sums = jnp.concatenate([added(keep[:2], up_low, down_low), added(keep[2:], up_high, down_high)])

    grad = total([at(sums, z, 0)] + [send(at(sums, (z + d) % 4, 0), along_z(d)) for d in (1, 3, 2)])

    moment1_out = decayed1 + 0.1 * grad
    moment2_out = decayed2 + 0.05 * grad * grad
    first_fix = 1.0 - 0.9**STEP
    second_fix = 1.0 - 0.95**STEP
    update = moment1_out / first_fix / (jnp.sqrt(moment2_out / second_fix) + 1e-08)
    master_out = master - 0.01 * (update + 0.1 * master)
    weight = master_out.astype(jnp.bfloat16)

    new_weight = gathered(scalars(dp), weight)
    return (new_weight, master_out, moment1_out, moment2_out)


def solution(mesh):
    in_specs = (P(AXES, None), P(AXES, None), P("fsdp", "dp"), P("fsdp", "dp"), P("fsdp", "dp"))
    out_specs = (P("fsdp", None), P("fsdp", "dp"), P("fsdp", "dp"), P("fsdp", "dp"))
    return jax.shard_map(step_of, mesh=mesh, in_specs=in_specs, out_specs=out_specs, check_vma=False)
```

profile of v0, /device:TPU:1, one launch (start us, length us, event | category | flops | bytes accessed | tf_op | source)
XLA Modules:
  0.0 134.6 jit_solution(17266416174897010475)
XLA Ops:
  1.3 11.8 %shard_map.85 = (bf16[4,4,128,512]{3,2,1,0:T(8,128)(2,1)}, bf16[3,4,4,128,512]{4,3,2,1,0:T(8,128)(2,1)}) custom-call(s32[2]{0:T(128)} %get-tuple-element.56.place_ref, bf16[768,1024]{1,0:T(8,128)(2,1)} %grad_ref.3, bf16[768,8192]{1,0:T(8,128)(2,1)} %second_ref.3, bf16[768,8192]{1,0:T(8,128)(2,1)} %second_ref.3), custom_call_target="tpu_custom_call" | custom-call | flops 6442450944 | bytes 6291456 | tf_op jit(solution)/shard_map/pallas_call | solution.py:91
  14.7 11.8 %shard_map.84 = (bf16[4,4,128,512]{3,2,1,0:T(8,128)(2,1)}, bf16[3,4,4,128,512]{4,3,2,1,0:T(8,128)(2,1)}) custom-call(s32[2]{0:T(128)} %get-tuple-element.55.place_ref, bf16[768,1024]{1,0:T(8,128)(2,1)} %grad_ref.3, bf16[768,8192]{1,0:T(8,128)(2,1)} %second_ref.3, bf16[768,8192]{1,0:T(8,128)(2,1)} %second_ref.3), custom_call_target="tpu_custom_call" | custom-call | flops 6442450944 | bytes 6291456 | tf_op jit(solution)/shard_map/pallas_call | solution.py:91
  27.6 2.4 %add_convert_fusion.3 = (bf16[2,4,128,512]{3,2,1,0:T(8,128)(2,1)S(1)}, bf16[2,4,128,512]{3,2,1,0:T(8,128)(2,1)S(1)}) fusion(bf16[4,4,128,512]{3,2,1,0:T(8,128)(2,1)S(1)} %collective-permute-done.1, bf16[4,4,128,512]{3,2,1,0:T(8,128)(2,1)} %get-tuple-element.24), kind=kLoop, calls=%fused_computation.8 | loop fusion | flops 4194304 | bytes 6291456 | tf_op jit(solution)/shard_map/convert_element_type | solution.py:226
  29.9 2.9 %collective-permute-start.3 = (bf16[2,4,128,512]{3,2,1,0:T(8,128)(2,1)S(1)}, bf16[2,4,128,512]{3,2,1,0:T(8,128)(2,1)S(1)}, u32[]{:S(2)}, u32[]{:S(2)}) collective-permute-start(bf16[2,4,128,512]{3,2,1,0:T(8,128)(2,1)S(1)} %get-tuple-element.47), channel_id=1, source_target_pairs={{0,96},{1,97},{2,98},{3,99},{8,11},{9,8},{10,9},{11,10},{4,100},{5... | collective-permute-start | bytes 3145736 | tf_op jit(solution)/shard_map/ppermute | solution.py:30
  32.8 2.2 %fusion.4 = (bf16[2,4,128,512]{3,2,1,0:T(8,128)(2,1)S(1)}, bf16[2,4,128,512]{3,2,1,0:T(8,128)(2,1)S(1)}) fusion(bf16[3,4,4,128,512]{4,3,2,1,0:T(8,128)(2,1)} %collective-permute-done, bf16[3,4,4,128,512]{4,3,2,1,0:T(8,128)(2,1)S(1)} %copy-done), kind=kLoop, calls=%fused_computation.11 | loop fusion | flops 4194304 | bytes 6291456 | tf_op jit(solution)/shard_map/convert_element_type | solution.py:226
  35.1 9.5 %collective-permute-done.3 = bf16[2,4,128,512]{3,2,1,0:T(8,128)(2,1)S(1)} collective-permute-done((bf16[2,4,128,512]{3,2,1,0:T(8,128)(2,1)S(1)}, bf16[2,4,128,512]{3,2,1,0:T(8,128)(2,1)S(1)}, u32[]{:S(2)}, u32[]{:S(2)}) %collective-permute-start.3) | collective-permute-done | bytes 1048608 | tf_op jit(solution)/shard_map/ppermute | solution.py:30
  44.6 3.4 %collective-permute-done.5 = bf16[2,4,128,512]{3,2,1,0:T(8,128)(2,1)S(1)} collective-permute-done((bf16[2,4,128,512]{3,2,1,0:T(8,128)(2,1)S(1)}, bf16[2,4,128,512]{3,2,1,0:T(8,128)(2,1)S(1)}, u32[]{:S(2)}, u32[]{:S(2)}) %collective-permute-start.5) | collective-permute-done | bytes 1048608 | tf_op jit(solution)/shard_map/ppermute | solution.py:30
  48.0 2.5 %fusion.1 = (bf16[2,4,128,512]{3,2,1,0:T(8,128)(2,1)S(1)}, bf16[2,4,128,512]{3,2,1,0:T(8,128)(2,1)S(1)}) fusion(bf16[2,4,128,512]{3,2,1,0:T(8,128)(2,1)S(1)} %collective-permute-done.5, bf16[3,4,4,128,512]{4,3,2,1,0:T(8,128)(2,1)} %collective-permute-done, bf16[3,4,4,128,512]{4,3,2,1,0:T(8,128)(2,1)S(1)} %copy-done, ...), kind=kLoop, calls=%fused_computation.3 | loop fusion | flops 6291456 | bytes 8388608 | tf_op jit(solution)/shard_map/convert_element_type | solution.py:226
  52.1 2.7 %collective-permute-start.7 = (bf16[2,4,128,512]{3,2,1,0:T(8,128)(2,1)S(1)}, bf16[2,4,128,512]{3,2,1,0:T(8,128)(2,1)S(1)}, u32[]{:S(2)}, u32[]{:S(2)}) collective-permute-start(bf16[2,4,128,512]{3,2,1,0:T(8,128)(2,1)S(1)} %get-tuple-element.44), channel_id=1, source_target_pairs={{0,96},{1,97},{2,98},{3,99},{8,11},{9,8},{10,9},{11,10},{4,100},{5... | collective-permute-start | bytes 3145736 | tf_op jit(solution)/shard_map/ppermute | solution.py:30
  54.7 2.3 %fusion.keep_ref = bf16[4,4,128,512]{3,2,1,0:T(8,128)(2,1)S(1)} fusion(bf16[3,4,4,128,512]{4,3,2,1,0:T(8,128)(2,1)} %collective-permute-done, bf16[3,4,4,128,512]{4,3,2,1,0:T(8,128)(2,1)S(1)} %copy-done), kind=kLoop, calls=%fused_computation.1 | loop fusion | flops 4194304 | bytes 6291456 | tf_op jit(solution)/shard_map/convert_element_type | solution.py:226
  57.0 7.5 %collective-permute-done.4.refs_1_ = bf16[2,4,128,512]{3,2,1,0:T(8,128)(2,1)S(1)} collective-permute-done((bf16[2,4,128,512]{3,2,1,0:T(8,128)(2,1)S(1)}, bf16[2,4,128,512]{3,2,1,0:T(8,128)(2,1)S(1)}, u32[]{:S(2)}, u32[]{:S(2)}) %collective-permute-start.4) | collective-permute-done | bytes 1048608 | tf_op jit(solution)/shard_map/ppermute | solution.py:30
  65.8 11.2 %collective-permute-done.2.refs_0_ = bf16[2,4,128,512]{3,2,1,0:T(8,128)(2,1)S(1)} collective-permute-done((bf16[2,4,128,512]{3,2,1,0:T(8,128)(2,1)S(1)}, bf16[2,4,128,512]{3,2,1,0:T(8,128)(2,1)S(1)}, u32[]{:S(2)}, u32[]{:S(2)}) %collective-permute-start.2) | collective-permute-done | bytes 1048608 | tf_op jit(solution)/shard_map/ppermute | solution.py:30
  78.7 2.2 %collective-permute-start.9 = (bf16[2,128,512]{2,1,0:T(8,128)(2,1)S(1)}, bf16[2,128,512]{2,1,0:T(8,128)(2,1)S(1)}, u32[]{:S(2)}, u32[]{:S(2)}) collective-permute-start(bf16[2,128,512]{2,1,0:T(8,128)(2,1)S(1)} %get-tuple-element.33), channel_id=1, source_target_pairs={{0,3},{1,0},{2,1},{3,2},{8,104},{9,105},{10,106},{11,107},{4,7},{5... | collective-permute-start | bytes 786440 | tf_op jit(solution)/shard_map/ppermute | solution.py:30
  80.9 2.7 %collective-permute-start.13 = (bf16[2,128,512]{2,1,0:T(8,128)(2,1)S(1)}, bf16[2,128,512]{2,1,0:T(8,128)(2,1)S(1)}, u32[]{:S(2)}, u32[]{:S(2)}) collective-permute-start(bf16[2,128,512]{2,1,0:T(8,128)(2,1)S(1)} %get-tuple-element.36), channel_id=1, source_target_pairs={{0,3},{1,0},{2,1},{3,2},{8,104},{9,105},{10,106},{11,107},{4,7},{5... | collective-permute-start | bytes 786440 | tf_op jit(solution)/shard_map/ppermute | solution.py:30
  84.4 3.1 %collective-permute-start.10 = (bf16[2,128,512]{2,1,0:T(8,128)(2,1)S(1)}, bf16[2,128,512]{2,1,0:T(8,128)(2,1)S(1)}, u32[]{:S(2)}, u32[]{:S(2)}) collective-permute-start(bf16[2,128,512]{2,1,0:T(8,128)(2,1)S(1)} %add_convert_fusion.8), channel_id=1, source_target_pairs={{0,3},{1,0},{2,1},{3,2},{8,104},{9,105},{10,106},{11,107},{4,7},{5... | collective-permute-start | bytes 786440 | tf_op jit(solution)/shard_map/ppermute | solution.py:30
  87.9 2.5 %collective-permute-done.8 = bf16[2,128,512]{2,1,0:T(8,128)(2,1)S(1)} collective-permute-done((bf16[2,128,512]{2,1,0:T(8,128)(2,1)S(1)}, bf16[2,128,512]{2,1,0:T(8,128)(2,1)S(1)}, u32[]{:S(2)}, u32[]{:S(2)}) %collective-permute-start.8) | collective-permute-done | bytes 262176 | tf_op jit(solution)/shard_map/ppermute | solution.py:30
  90.8 3.5 %collective-permute-done.12 = bf16[2,128,512]{2,1,0:T(8,128)(2,1)S(1)} collective-permute-done((bf16[2,128,512]{2,1,0:T(8,128)(2,1)S(1)}, bf16[2,128,512]{2,1,0:T(8,128)(2,1)S(1)}, u32[]{:S(2)}, u32[]{:S(2)}) %collective-permute-start.12) | collective-permute-done | bytes 262176 | tf_op jit(solution)/shard_map/ppermute | solution.py:30
  96.4 2.2 %collective-permute-start.15 = (bf16[128,512]{1,0:T(8,128)(2,1)S(1)}, bf16[128,512]{1,0:T(8,128)(2,1)S(1)}, u32[]{:S(2)}, u32[]{:S(2)}) collective-permute-start(bf16[128,512]{1,0:T(8,128)(2,1)S(1)} %get-tuple-element.49), channel_id=1, source_target_pairs={{0,20},{1,21},{2,22},{3,23},{8,28},{9,29},{10,30},{11,31},{4,0},{5... | collective-permute-start | bytes 393224 | tf_op jit(solution)/shard_map/ppermute | solution.py:30
  100.9 3.0 %collective-permute-done.16 = bf16[128,512]{1,0:T(8,128)(2,1)S(1)} collective-permute-done((bf16[128,512]{1,0:T(8,128)(2,1)S(1)}, bf16[128,512]{1,0:T(8,128)(2,1)S(1)}, u32[]{:S(2)}, u32[]{:S(2)}) %collective-permute-start.16) | collective-permute-done | bytes 131104 | tf_op jit(solution)/shard_map/ppermute | solution.py:30
  105.1 6.7 %collective-permute-start.17 = (bf16[128,512]{1,0:T(8,128)(2,1)S(1)}, bf16[128,512]{1,0:T(8,128)(2,1)S(1)}, u32[]{:S(2)}, u32[]{:S(2)}) collective-permute-start(bf16[128,512]{1,0:T(8,128)(2,1)S(1)} %get-tuple-element.38), channel_id=1, source_target_pairs={{0,8},{1,9},{2,10},{3,11},{8,0},{9,1},{10,2},{11,3},{4,12},{5,13},... | collective-permute-start | bytes 393224 | tf_op jit(solution)/shard_map/ppermute | solution.py:30
  112.9 2.0 %collective-permute-start.19 = (bf16[2,128,512]{2,1,0:T(8,128)(2,1)S(1)}, bf16[2,128,512]{2,1,0:T(8,128)(2,1)S(1)}, u32[]{:S(2)}, u32[]{:S(2)}) collective-permute-start(bf16[2,128,512]{2,1,0:T(8,128)(2,1)S(1)} %pad_maximum_fusion.refs_0_), channel_id=1, source_target_pairs={{0,48},{1,49},{2,50},{3,51},{8,120},{9,121},{10,122},{11,123},{4,5... | collective-permute-start | bytes 786440 | tf_op jit(solution)/shard_map/ppermute | solution.py:30
  114.9 3.7 %collective-permute-start.20 = (bf16[2,128,512]{2,1,0:T(8,128)(2,1)S(1)}, bf16[2,128,512]{2,1,0:T(8,128)(2,1)S(1)}, u32[]{:S(2)}, u32[]{:S(2)}) collective-permute-start(bf16[2,128,512]{2,1,0:T(8,128)(2,1)S(1)} %pad_maximum_fusion.refs_0_), channel_id=1, source_target_pairs={{0,64},{1,65},{2,66},{3,67},{8,88},{9,89},{10,90},{11,91},{4,68},{... | collective-permute-start | bytes 786440 | tf_op jit(solution)/shard_map/ppermute | solution.py:30
  121.0 2.8 %collective-permute-done.19.refs_2_ = bf16[2,128,512]{2,1,0:T(8,128)(2,1)S(1)} collective-permute-done((bf16[2,128,512]{2,1,0:T(8,128)(2,1)S(1)}, bf16[2,128,512]{2,1,0:T(8,128)(2,1)S(1)}, u32[]{:S(2)}, u32[]{:S(2)}) %collective-permute-start.19) | collective-permute-done | bytes 262176 | tf_op jit(solution)/shard_map/ppermute | solution.py:30
  123.8 7.5 %collective-permute-start.23 = (bf16[2,128,512]{2,1,0:T(8,128)(2,1)S(1)}, bf16[2,128,512]{2,1,0:T(8,128)(2,1)S(1)}, u32[]{:S(2)}, u32[]{:S(2)}) collective-permute-start(bf16[2,128,512]{2,1,0:T(8,128)(2,1)S(1)} %collective-permute-done.19.refs_2_), channel_id=1, source_target_pairs={{0,8},{1,9},{2,10},{3,11},{8,0},{9,1},{10,2},{11,3},{4,12},{5,13},... | collective-permute-start | bytes 786440 | tf_op jit(solution)/shard_map/ppermute | solution.py:30
  (52 shorter events, 21.6 us)
Async XLA Ops:
  13.1 19.7 %collective-permute-start = (bf16[3,4,4,128,512]{4,3,2,1,0:T(8,128)(2,1)}, bf16[3,4,4,128,512]{4,3,2,1,0:T(8,128)(2,1)}, u32[]{:S(2)}, u32[]{:S(2)}) collective-permute-start(bf16[3,4,4,128,512]{4,3,2,1,0:T(8,128)(2,1)} %get-tuple-element.23), channel_id=1, source_target_pairs={{0,8},{1,9},{2,10},{3,11},{8,0},{9,1},{10,2},{11,3},{4,12},{5,13},... | collective-permute-start | bytes 18874376 | tf_op jit(solution)/shard_map/ppermute | solution.py:30
  14.6 13.0 %collective-permute-start.1 = (bf16[4,4,128,512]{3,2,1,0:T(8,128)(2,1)}, bf16[4,4,128,512]{3,2,1,0:T(8,128)(2,1)S(1)}, u32[]{:S(2)}, u32[]{:S(2)}) collective-permute-start(bf16[4,4,128,512]{3,2,1,0:T(8,128)(2,1)} %get-tuple-element.25), channel_id=1, source_target_pairs={{0,8},{1,9},{2,10},{3,11},{8,0},{9,1},{10,2},{11,3},{4,12},{5,13},... | collective-permute-start | bytes 6291464 | tf_op jit(solution)/shard_map/ppermute | solution.py:30
  29.9 14.7 %collective-permute-start.3 = (bf16[2,4,128,512]{3,2,1,0:T(8,128)(2,1)S(1)}, bf16[2,4,128,512]{3,2,1,0:T(8,128)(2,1)S(1)}, u32[]{:S(2)}, u32[]{:S(2)}) collective-permute-start(bf16[2,4,128,512]{3,2,1,0:T(8,128)(2,1)S(1)} %get-tuple-element.47), channel_id=1, source_target_pairs={{0,96},{1,97},{2,98},{3,99},{8,11},{9,8},{10,9},{11,10},{4,100},{5... | collective-permute-start | bytes 3145736 | tf_op jit(solution)/shard_map/ppermute | solution.py:30
  32.8 15.2 %collective-permute-start.5 = (bf16[2,4,128,512]{3,2,1,0:T(8,128)(2,1)S(1)}, bf16[2,4,128,512]{3,2,1,0:T(8,128)(2,1)S(1)}, u32[]{:S(2)}, u32[]{:S(2)}) collective-permute-start(bf16[2,4,128,512]{3,2,1,0:T(8,128)(2,1)S(1)} %get-tuple-element.46), channel_id=1, source_target_pairs={{0,32},{1,33},{2,34},{3,35},{8,9},{9,10},{10,11},{11,8},{4,36},{5,... | collective-permute-start | bytes 3145736 | tf_op jit(solution)/shard_map/ppermute | solution.py:30
  50.5 14.0 %collective-permute-start.4 = (bf16[2,4,128,512]{3,2,1,0:T(8,128)(2,1)S(1)}, bf16[2,4,128,512]{3,2,1,0:T(8,128)(2,1)S(1)}, u32[]{:S(2)}, u32[]{:S(2)}) collective-permute-start(bf16[2,4,128,512]{3,2,1,0:T(8,128)(2,1)S(1)} %get-tuple-element.43), channel_id=1, source_target_pairs={{0,96},{1,97},{2,98},{3,99},{8,11},{9,8},{10,9},{11,10},{4,100},{5... | collective-permute-start | bytes 3145736 | tf_op jit(solution)/shard_map/ppermute | solution.py:30
  50.6 15.2 %collective-permute-start.6 = (bf16[2,4,128,512]{3,2,1,0:T(8,128)(2,1)S(1)}, bf16[2,4,128,512]{3,2,1,0:T(8,128)(2,1)S(1)}, u32[]{:S(2)}, u32[]{:S(2)}) collective-permute-start(bf16[2,4,128,512]{3,2,1,0:T(8,128)(2,1)S(1)} %get-tuple-element.42), channel_id=1, source_target_pairs={{0,32},{1,33},{2,34},{3,35},{8,9},{9,10},{10,11},{11,8},{4,36},{5,... | collective-permute-start | bytes 3145736 | tf_op jit(solution)/shard_map/ppermute | solution.py:30
  52.0 25.0 %collective-permute-start.2 = (bf16[2,4,128,512]{3,2,1,0:T(8,128)(2,1)S(1)}, bf16[2,4,128,512]{3,2,1,0:T(8,128)(2,1)S(1)}, u32[]{:S(2)}, u32[]{:S(2)}) collective-permute-start(bf16[2,4,128,512]{3,2,1,0:T(8,128)(2,1)S(1)} %get-tuple-element.45), channel_id=1, source_target_pairs={{0,32},{1,33},{2,34},{3,35},{8,9},{9,10},{10,11},{11,8},{4,36},{5,... | collective-permute-start | bytes 3145736 | tf_op jit(solution)/shard_map/ppermute | solution.py:30
  52.1 25.0 %collective-permute-start.7 = (bf16[2,4,128,512]{3,2,1,0:T(8,128)(2,1)S(1)}, bf16[2,4,128,512]{3,2,1,0:T(8,128)(2,1)S(1)}, u32[]{:S(2)}, u32[]{:S(2)}) collective-permute-start(bf16[2,4,128,512]{3,2,1,0:T(8,128)(2,1)S(1)} %get-tuple-element.44), channel_id=1, source_target_pairs={{0,96},{1,97},{2,98},{3,99},{8,11},{9,8},{10,9},{11,10},{4,100},{5... | collective-permute-start | bytes 3145736 | tf_op jit(solution)/shard_map/ppermute | solution.py:30
  78.7 5.6 %collective-permute-start.9 = (bf16[2,128,512]{2,1,0:T(8,128)(2,1)S(1)}, bf16[2,128,512]{2,1,0:T(8,128)(2,1)S(1)}, u32[]{:S(2)}, u32[]{:S(2)}) collective-permute-start(bf16[2,128,512]{2,1,0:T(8,128)(2,1)S(1)} %get-tuple-element.33), channel_id=1, source_target_pairs={{0,3},{1,0},{2,1},{3,2},{8,104},{9,105},{10,106},{11,107},{4,7},{5... | collective-permute-start | bytes 786440 | tf_op jit(solution)/shard_map/ppermute | solution.py:30
  80.9 6.6 %collective-permute-start.11 = (bf16[2,128,512]{2,1,0:T(8,128)(2,1)S(1)}, bf16[2,128,512]{2,1,0:T(8,128)(2,1)S(1)}, u32[]{:S(2)}, u32[]{:S(2)}) collective-permute-start(bf16[2,128,512]{2,1,0:T(8,128)(2,1)S(1)} %get-tuple-element.35), channel_id=1, source_target_pairs={{0,1},{1,2},{2,3},{3,0},{8,40},{9,41},{10,42},{11,43},{4,5},{5,6},... | collective-permute-start | bytes 786440 | tf_op jit(solution)/shard_map/ppermute | solution.py:30
  80.9 7.0 %collective-permute-start.13 = (bf16[2,128,512]{2,1,0:T(8,128)(2,1)S(1)}, bf16[2,128,512]{2,1,0:T(8,128)(2,1)S(1)}, u32[]{:S(2)}, u32[]{:S(2)}) collective-permute-start(bf16[2,128,512]{2,1,0:T(8,128)(2,1)S(1)} %get-tuple-element.36), channel_id=1, source_target_pairs={{0,3},{1,0},{2,1},{3,2},{8,104},{9,105},{10,106},{11,107},{4,7},{5... | collective-permute-start | bytes 786440 | tf_op jit(solution)/shard_map/ppermute | solution.py:30
  83.5 6.9 %collective-permute-start.8 = (bf16[2,128,512]{2,1,0:T(8,128)(2,1)S(1)}, bf16[2,128,512]{2,1,0:T(8,128)(2,1)S(1)}, u32[]{:S(2)}, u32[]{:S(2)}) collective-permute-start(bf16[2,128,512]{2,1,0:T(8,128)(2,1)S(1)} %get-tuple-element.31), channel_id=1, source_target_pairs={{0,1},{1,2},{2,3},{3,0},{8,40},{9,41},{10,42},{11,43},{4,5},{5,6},... | collective-permute-start | bytes 786440 | tf_op jit(solution)/shard_map/ppermute | solution.py:30
  84.4 6.4 %collective-permute-start.10 = (bf16[2,128,512]{2,1,0:T(8,128)(2,1)S(1)}, bf16[2,128,512]{2,1,0:T(8,128)(2,1)S(1)}, u32[]{:S(2)}, u32[]{:S(2)}) collective-permute-start(bf16[2,128,512]{2,1,0:T(8,128)(2,1)S(1)} %add_convert_fusion.8), channel_id=1, source_target_pairs={{0,3},{1,0},{2,1},{3,2},{8,104},{9,105},{10,106},{11,107},{4,7},{5... | collective-permute-start | bytes 786440 | tf_op jit(solution)/shard_map/ppermute | solution.py:30
  87.5 6.8 %collective-permute-start.12 = (bf16[2,128,512]{2,1,0:T(8,128)(2,1)S(1)}, bf16[2,128,512]{2,1,0:T(8,128)(2,1)S(1)}, u32[]{:S(2)}, u32[]{:S(2)}) collective-permute-start(bf16[2,128,512]{2,1,0:T(8,128)(2,1)S(1)} %add_convert_fusion.6), channel_id=1, source_target_pairs={{0,1},{1,2},{2,3},{3,0},{8,40},{9,41},{10,42},{11,43},{4,5},{5,6},... | collective-permute-start | bytes 786440 | tf_op jit(solution)/shard_map/ppermute | solution.py:30
  94.7 6.2 %collective-permute-start.14 = (bf16[128,512]{1,0:T(8,128)(2,1)S(1)}, bf16[128,512]{1,0:T(8,128)(2,1)S(1)}, u32[]{:S(2)}, u32[]{:S(2)}) collective-permute-start(bf16[128,512]{1,0:T(8,128)(2,1)S(1)} %get-tuple-element.48), channel_id=1, source_target_pairs={{0,4},{1,5},{2,6},{3,7},{8,12},{9,13},{10,14},{11,15},{4,16},{5,17... | collective-permute-start | bytes 393224 | tf_op jit(solution)/shard_map/ppermute | solution.py:30
  96.4 4.5 %collective-permute-start.15 = (bf16[128,512]{1,0:T(8,128)(2,1)S(1)}, bf16[128,512]{1,0:T(8,128)(2,1)S(1)}, u32[]{:S(2)}, u32[]{:S(2)}) collective-permute-start(bf16[128,512]{1,0:T(8,128)(2,1)S(1)} %get-tuple-element.49), channel_id=1, source_target_pairs={{0,20},{1,21},{2,22},{3,23},{8,28},{9,29},{10,30},{11,31},{4,0},{5... | collective-permute-start | bytes 393224 | tf_op jit(solution)/shard_map/ppermute | solution.py:30
  98.6 5.3 %collective-permute-start.16 = (bf16[128,512]{1,0:T(8,128)(2,1)S(1)}, bf16[128,512]{1,0:T(8,128)(2,1)S(1)}, u32[]{:S(2)}, u32[]{:S(2)}) collective-permute-start(bf16[128,512]{1,0:T(8,128)(2,1)S(1)} %get-tuple-element.50), channel_id=1, source_target_pairs={{0,16},{1,17},{2,18},{3,19},{8,24},{9,25},{10,26},{11,27},{4,20},{... | collective-permute-start | bytes 393224 | tf_op jit(solution)/shard_map/ppermute | solution.py:30
  105.1 7.6 %collective-permute-start.17 = (bf16[128,512]{1,0:T(8,128)(2,1)S(1)}, bf16[128,512]{1,0:T(8,128)(2,1)S(1)}, u32[]{:S(2)}, u32[]{:S(2)}) collective-permute-start(bf16[128,512]{1,0:T(8,128)(2,1)S(1)} %get-tuple-element.38), channel_id=1, source_target_pairs={{0,8},{1,9},{2,10},{3,11},{8,0},{9,1},{10,2},{11,3},{4,12},{5,13},... | collective-permute-start | bytes 393224 | tf_op jit(solution)/shard_map/ppermute | solution.py:30
  112.8 7.2 %collective-permute-start.18 = (bf16[2,128,512]{2,1,0:T(8,128)(2,1)S(1)}, bf16[2,128,512]{2,1,0:T(8,128)(2,1)S(1)}, u32[]{:S(2)}, u32[]{:S(2)}) collective-permute-start(bf16[2,128,512]{2,1,0:T(8,128)(2,1)S(1)} %pad_maximum_fusion.refs_0_), channel_id=1, source_target_pairs={{0,32},{1,33},{2,34},{3,35},{8,104},{9,105},{10,106},{11,107},{4,3... | collective-permute-start | bytes 786440 | tf_op jit(solution)/shard_map/ppermute | solution.py:30
  112.9 10.9 %collective-permute-start.19 = (bf16[2,128,512]{2,1,0:T(8,128)(2,1)S(1)}, bf16[2,128,512]{2,1,0:T(8,128)(2,1)S(1)}, u32[]{:S(2)}, u32[]{:S(2)}) collective-permute-start(bf16[2,128,512]{2,1,0:T(8,128)(2,1)S(1)} %pad_maximum_fusion.refs_0_), channel_id=1, source_target_pairs={{0,48},{1,49},{2,50},{3,51},{8,120},{9,121},{10,122},{11,123},{4,5... | collective-permute-start | bytes 786440 | tf_op jit(solution)/shard_map/ppermute | solution.py:30
  114.9 16.4 %collective-permute-start.20 = (bf16[2,128,512]{2,1,0:T(8,128)(2,1)S(1)}, bf16[2,128,512]{2,1,0:T(8,128)(2,1)S(1)}, u32[]{:S(2)}, u32[]{:S(2)}) collective-permute-start(bf16[2,128,512]{2,1,0:T(8,128)(2,1)S(1)} %pad_maximum_fusion.refs_0_), channel_id=1, source_target_pairs={{0,64},{1,65},{2,66},{3,67},{8,88},{9,89},{10,90},{11,91},{4,68},{... | collective-permute-start | bytes 786440 | tf_op jit(solution)/shard_map/ppermute | solution.py:30
  118.5 12.8 %collective-permute-start.21 = (bf16[128,512]{1,0:T(8,128)(2,1)S(1)}, bf16[128,512]{1,0:T(8,128)(2,1)S(1)}, u32[]{:S(2)}, u32[]{:S(2)}) collective-permute-start(bf16[128,512]{1,0:T(8,128)(2,1)S(1)} %get-tuple-element.38), channel_id=1, source_target_pairs={{0,16},{1,17},{2,18},{3,19},{8,24},{9,25},{10,26},{11,27},{4,20},{... | collective-permute-start | bytes 393224 | tf_op jit(solution)/shard_map/ppermute | solution.py:30
  120.0 13.0 %collective-permute-start.22 = (bf16[2,128,512]{2,1,0:T(8,128)(2,1)S(1)}, bf16[2,128,512]{2,1,0:T(8,128)(2,1)S(1)}, u32[]{:S(2)}, u32[]{:S(2)}) collective-permute-start(bf16[2,128,512]{2,1,0:T(8,128)(2,1)S(1)} %collective-permute-done.18.refs_1_), channel_id=1, source_target_pairs={{0,8},{1,9},{2,10},{3,11},{8,0},{9,1},{10,2},{11,3},{4,12},{5,13},... | collective-permute-start | bytes 786440 | tf_op jit(solution)/shard_map/ppermute | solution.py:30
  123.8 9.2 %collective-permute-start.23 = (bf16[2,128,512]{2,1,0:T(8,128)(2,1)S(1)}, bf16[2,128,512]{2,1,0:T(8,128)(2,1)S(1)}, u32[]{:S(2)}, u32[]{:S(2)}) collective-permute-start(bf16[2,128,512]{2,1,0:T(8,128)(2,1)S(1)} %collective-permute-done.19.refs_2_), channel_id=1, source_target_pairs={{0,8},{1,9},{2,10},{3,11},{8,0},{9,1},{10,2},{11,3},{4,12},{5,13},... | collective-permute-start | bytes 786440 | tf_op jit(solution)/shard_map/ppermute | solution.py:30
  (6 other events, 55.8 us)
where the time goes:
time: 135 us
  waiting for transfers between devices  50.3 us (37%)
  starting transfers between devices  44.8 us (33%)
  Pallas kernels  26.6 us (20%)
  other arithmetic  11.8 us (9%)
    ppermute x26, waiting for transfers between devices, send(): return lax.ppermute(value, AXES, moved(step))  50.3 us
    ppermute x26, starting transfers between devices, send(): return lax.ppermute(value, AXES, moved(step))  44.8 us
    pallas_call x2, Pallas kernels, products(): pl.pallas_call(functools.partial(product_kernel, scale), grid_spec=pltpu....  23.5 us
    convert_element_type x7, other arithmetic, added(): return total(values).astype(jnp.bfloat16)  9.69 us
  transfers between devices with their start and end apart: 26, of which 15 were waited for; matrix products, arithmetic and copies ran while one was open for 5% of the time, Pallas kernels for 9%

commit v1 on v0

--- a/solution.py
+++ b/solution.py
@@ -46,43 +46,27 @@
     return lambda c: (0, d, 0, 0)
 
 
-def product_kernel(scale, place_ref, grad_ref, first_ref, second_ref, far_ref, rest_ref, buf, sems):
+def product_kernel(scale, place_ref, grad_ref, first_ref, second_ref, far_ref, rest_ref):
     step = pl.program_id(0)
-    slot = step % 2
     first = place_ref[0] == 0
-
-    def each(step, slot, act):
-        for y in range(4):
-            one, other = jnp.where(first, step, y), jnp.where(first, y, step)
-            hops = (one - place_ref[1]) & 3
-
-            @pl.when(hops == 2)
-            def _():
-                act(pltpu.make_async_copy(buf.at[slot, y], far_ref.at[other], sems.at[slot, y]))
-
-            @pl.when(hops != 2)
-            def _():
-                target = rest_ref.at[jnp.where(hops == 0, 2, hops >> 1), other]
-                act(pltpu.make_async_copy(buf.at[slot, y], target, sems.at[slot, y]))
-
-    @pl.when(step >= 2)
-    def _():
-        each(step - 2, slot, lambda copy: copy.wait())
-
     for i, act_ref in enumerate((first_ref, second_ref)):
         value = lax.dot_general(
             grad_ref[...], act_ref[...], (((0,), (0,)), ((), ())), preferred_element_type=jnp.float32
         )
         value = (value * scale).astype(jnp.bfloat16).reshape(2, 4, 128, 512)
-        for low in range(2):
-            for y in range(4):
-                buf[slot, y, 2 * i + low] = value[low, y]
-    each(step, slot, lambda copy: copy.start())
-
-    @pl.when(step == 3)
-    def _():
-        each(step - 1, 1 - slot, lambda copy: copy.wait())
-        each(step, slot, lambda copy: copy.wait())
+        for y in range(4):
+            one, other = jnp.where(first, step, y), jnp.where(first, y, step)
+            hops = (one - place_ref[1]) & 3
+
+            @pl.when(hops == 2)
+            def _():
+                for low in range(2):
+                    far_ref[other, 2 * i + low] = value[low, y]
+
+            @pl.when(hops != 2)
+            def _():
+                for low in range(2):
+                    rest_ref[jnp.where(hops == 0, 2, hops >> 1), other, 2 * i + low] = value[low, y]
 
 
 def products(place, out_grad, act, scale):
@@ -98,18 +82,16 @@
                 pl.BlockSpec((tokens, 512), lambda k, h: (0, 4 * k + h[0])),
                 pl.BlockSpec((tokens, 512), lambda k, h: (0, 4 * k + 2 + h[0])),
             ],
-            out_specs=[pl.BlockSpec(memory_space=pl.ANY)] * 2,
-            scratch_shapes=[
-                pltpu.VMEM((2, 4, 4, 128, 512), jnp.bfloat16),
-                pltpu.SemaphoreType.DMA((2, 4)),
-            ],
+            out_specs=[pl.BlockSpec(memory_space=pltpu.VMEM)] * 2,
         ),
-        out_shape=[jax.ShapeDtypeStruct(s, jnp.bfloat16) for s in shapes],
-        compiler_params=pltpu.CompilerParams(dimension_semantics=("arbitrary",)),
+        out_shape=[pltpu.VMEM(s, jnp.bfloat16) for s in shapes],
+        compiler_params=pltpu.CompilerParams(
+            dimension_semantics=("arbitrary",), vmem_limit_bytes=28 * 2**20
+        ),
         cost_estimate=pl.CostEstimate(
             flops=2 * 1024 * tokens * 4096, bytes_accessed=tokens * 8192, transcendentals=0
         ),
-    )(place, out_grad, act, act)
+    )(place, out_grad, *[pltpu.with_memory_space_constraint(act, pltpu.HBM)] * 2)
 
 
 def fold_kernel(two_ref, keep_ref, *refs):
@@ -165,8 +147,8 @@
         place(ins[0].at[i], x, zh, c ^ i)
         for owner, held in ((c, ins[1:5]), (1 - c, ins[5:9])):
             side = x + 3 + 2 * owner
-            place(held[0].at[i], side, zh, owner ^ i)
-            place(held[1].at[i], side, 1 - zh, owner ^ i)
+            place(held[0].at[i], side, zh ^ owner, owner ^ i)
+            place(held[1].at[i], side, 1 - (zh ^ owner), owner ^ i)
             place(held[2].at[i], x + 2, zh ^ owner, owner ^ i)
             if i == 0:
                 place(held[3], x, 1 - zh, owner)
@@ -191,10 +173,11 @@
 def gathered(dp, weight):
     over = send(weight, lambda c: (0, 2, 0, 0))
     both = jnp.stack([weight, swap_cores(weight)])
+    near = send(both, lambda c: (1 - 2 * c, 2 * c, 0, 0))
     held = [
-        send(both, lambda c: (1 - 2 * c, 0, 0, 0)),
-        send(both, lambda c: (1 - 2 * c, 2, 0, 0)),
-        send(both, lambda c: (2, 2 * c, 0, 0)),
+        near,
+        send(both, lambda c: (1 - 2 * c, 2 - 2 * c, 0, 0)),
+        send(near, lambda c: (1 - 2 * c, 0, 0, 0)),
         over,
     ]
     return assemble(dp, both, *held, *(swap_cores(v) for v in held))

time: 135 us -> 129 us (0.956)
  starting transfers between devices: 44.8 us -> 37.3 us
  other arithmetic: 11.8 us -> 4.88 us
  waiting for transfers between devices: 50.3 us -> 57 us
  local copies, waits for them, and re-layouts: 0.02 us -> 1.43 us
    ppermute x26, starting transfers between devices: 44.8 us -> 37.3 us  [send(): return lax.ppermute(value, AXES, moved(step))]
    ppermute x26, waiting for transfers between devices: 50.3 us -> 57 us  [send(): return lax.ppermute(value, AXES, moved(step))]
    convert_element_type x7, other arithmetic: 9.69 us -> 3.35 us  [added(): return total(values).astype(jnp.bfloat16)]
    unnamed x8 -> x10, local copies, waits for them, and re-layouts: 0.02 us -> 1.43 us
  transfers between devices with their start and end apart: 26 -> 26, of which waited for: 15 -> 16; matrix products, arithmetic and copies ran while one was open for 5% -> 2% of each run, Pallas kernels for 9% -> 9%
where the time goes in v1:
time: 129 us
  waiting for transfers between devices  57 us (44%)
  starting transfers between devices  37.3 us (29%)
  Pallas kernels  27 us (21%)
  other arithmetic  4.88 us (4%)
  local copies, waits for them, and re-layouts  1.43 us (1%)
    ppermute x26, waiting for transfers between devices, send(): return lax.ppermute(value, AXES, moved(step))  57 us
    ppermute x26, starting transfers between devices, send(): return lax.ppermute(value, AXES, moved(step))  37.3 us
    pallas_call x2, Pallas kernels, products(): pl.pallas_call(functools.partial(product_kernel, scale), grid_spec=pltpu....  23.9 us
    convert_element_type x7, other arithmetic, added(): return total(values).astype(jnp.bfloat16)  3.35 us
  transfers between devices with their start and end apart: 26, of which 16 were waited for; matrix products, arithmetic and copies ran while one was open for 2% of the time, Pallas kernels for 9%

profile of v1, /device:TPU:1, one launch (start us, length us, event | category | flops | bytes accessed | tf_op | source)
XLA Modules:
  0.0 128.8 jit_solution(16638190618159837312)
XLA Ops:
  2.2 12.0 %shard_map.85 = (bf16[4,4,128,512]{3,2,1,0:T(8,128)(2,1)S(1)}, bf16[3,4,4,128,512]{4,3,2,1,0:T(8,128)(2,1)S(1)}) custom-call(s32[2]{0:T(128)S(1)} %get-tuple-element.56.place_ref, bf16[768,1024]{1,0:T(8,128)(2,1)S(1)} %copy-done, bf16[768,8192]{1,0:T(8,128)(2,1)} %second_ref.3, bf16[768,8192]{1,0:T(8,128)(2,1)} %second_ref.3), custom_call_target="tpu_custom_call" | custom-call | flops 6442450944 | bytes 6291456 | tf_op jit(solution)/shard_map/pallas_call | solution.py:75
  14.1 1.5 %collective-permute-start = (bf16[3,4,4,128,512]{4,3,2,1,0:T(8,128)(2,1)S(1)}, bf16[3,4,4,128,512]{4,3,2,1,0:T(8,128)(2,1)S(1)}, u32[]{:S(2)}, u32[]{:S(2)}) collective-permute-start(bf16[3,4,4,128,512]{4,3,2,1,0:T(8,128)(2,1)S(1)} %get-tuple-element.23), channel_id=1, source_target_pairs={{0,8},{1,9},{2,10},{3,11},{8,0},{9,1},{10,2},{11,3},{4,12},{5,13},... | collective-permute-start | bytes 18874376 | tf_op jit(solution)/shard_map/ppermute | solution.py:30
  15.7 12.0 %shard_map.84 = (bf16[4,4,128,512]{3,2,1,0:T(8,128)(2,1)S(1)}, bf16[3,4,4,128,512]{4,3,2,1,0:T(8,128)(2,1)S(1)}) custom-call(s32[2]{0:T(128)S(1)} %get-tuple-element.55.place_ref, bf16[768,1024]{1,0:T(8,128)(2,1)S(1)} %copy-done.1, bf16[768,8192]{1,0:T(8,128)(2,1)} %second_ref.3, bf16[768,8192]{1,0:T(8,128)(2,1)} %second_ref.3), custom_call_target="tpu_custom_call" | custom-call | flops 6442450944 | bytes 6291456 | tf_op jit(solution)/shard_map/pallas_call | solution.py:75
  29.1 2.9 %collective-permute-start.3 = (bf16[2,4,128,512]{3,2,1,0:T(8,128)(2,1)S(1)}, bf16[2,4,128,512]{3,2,1,0:T(8,128)(2,1)S(1)}, u32[]{:S(2)}, u32[]{:S(2)}) collective-permute-start(bf16[2,4,128,512]{3,2,1,0:T(8,128)(2,1)S(1)} %get-tuple-element.47), channel_id=1, source_target_pairs={{0,96},{1,97},{2,98},{3,99},{8,11},{9,8},{10,9},{11,10},{4,100},{5... | collective-permute-start | bytes 3145736 | tf_op jit(solution)/shard_map/ppermute | solution.py:30
  32.7 11.0 %collective-permute-done.3 = bf16[2,4,128,512]{3,2,1,0:T(8,128)(2,1)S(1)} collective-permute-done((bf16[2,4,128,512]{3,2,1,0:T(8,128)(2,1)S(1)}, bf16[2,4,128,512]{3,2,1,0:T(8,128)(2,1)S(1)}, u32[]{:S(2)}, u32[]{:S(2)}) %collective-permute-start.3) | collective-permute-done | bytes 1048608 | tf_op jit(solution)/shard_map/ppermute | solution.py:30
  43.7 3.4 %collective-permute-done.5 = bf16[2,4,128,512]{3,2,1,0:T(8,128)(2,1)S(1)} collective-permute-done((bf16[2,4,128,512]{3,2,1,0:T(8,128)(2,1)S(1)}, bf16[2,4,128,512]{3,2,1,0:T(8,128)(2,1)S(1)}, u32[]{:S(2)}, u32[]{:S(2)}) %collective-permute-start.5) | collective-permute-done | bytes 1048608 | tf_op jit(solution)/shard_map/ppermute | solution.py:30
  48.2 1.5 %collective-permute-start.6 = (bf16[2,4,128,512]{3,2,1,0:T(8,128)(2,1)S(1)}, bf16[2,4,128,512]{3,2,1,0:T(8,128)(2,1)S(1)}, u32[]{:S(2)}, u32[]{:S(2)}) collective-permute-start(bf16[2,4,128,512]{3,2,1,0:T(8,128)(2,1)S(1)} %get-tuple-element.42), channel_id=1, source_target_pairs={{0,32},{1,33},{2,34},{3,35},{8,9},{9,10},{10,11},{11,8},{4,36},{5,... | collective-permute-start | bytes 3145736 | tf_op jit(solution)/shard_map/ppermute | solution.py:30
  49.7 2.7 %collective-permute-start.7 = (bf16[2,4,128,512]{3,2,1,0:T(8,128)(2,1)S(1)}, bf16[2,4,128,512]{3,2,1,0:T(8,128)(2,1)S(1)}, u32[]{:S(2)}, u32[]{:S(2)}) collective-permute-start(bf16[2,4,128,512]{3,2,1,0:T(8,128)(2,1)S(1)} %get-tuple-element.44), channel_id=1, source_target_pairs={{0,96},{1,97},{2,98},{3,99},{8,11},{9,8},{10,9},{11,10},{4,100},{5... | collective-permute-start | bytes 3145736 | tf_op jit(solution)/shard_map/ppermute | solution.py:30
  53.0 9.1 %collective-permute-done.4.refs_1_ = bf16[2,4,128,512]{3,2,1,0:T(8,128)(2,1)S(1)} collective-permute-done((bf16[2,4,128,512]{3,2,1,0:T(8,128)(2,1)S(1)}, bf16[2,4,128,512]{3,2,1,0:T(8,128)(2,1)S(1)}, u32[]{:S(2)}, u32[]{:S(2)}) %collective-permute-start.4) | collective-permute-done | bytes 1048608 | tf_op jit(solution)/shard_map/ppermute | solution.py:30
  63.4 11.2 %collective-permute-done.2.refs_0_ = bf16[2,4,128,512]{3,2,1,0:T(8,128)(2,1)S(1)} collective-permute-done((bf16[2,4,128,512]{3,2,1,0:T(8,128)(2,1)S(1)}, bf16[2,4,128,512]{3,2,1,0:T(8,128)(2,1)S(1)}, u32[]{:S(2)}, u32[]{:S(2)}) %collective-permute-start.2) | collective-permute-done | bytes 1048608 | tf_op jit(solution)/shard_map/ppermute | solution.py:30
  74.7 1.6 %shard_map.86 = (bf16[2,128,512]{2,1,0:T(8,128)(2,1)S(1)}, bf16[2,128,512]{2,1,0:T(8,128)(2,1)S(1)}, bf16[2,128,512]{2,1,0:T(8,128)(2,1)S(1)}, bf16[2,128,512]{2...) custom-call(s32[1]{0:T(128)} %bitcast.1.two_ref, ...), custom_call_target="tpu_custom_call" | custom-call | flops 16777216 | bytes 8388608 | tf_op jit(solution)/shard_map/pallas_call | solution.py:124
  76.3 2.2 %collective-permute-start.9 = (bf16[2,128,512]{2,1,0:T(8,128)(2,1)S(1)}, bf16[2,128,512]{2,1,0:T(8,128)(2,1)S(1)}, u32[]{:S(2)}, u32[]{:S(2)}) collective-permute-start(bf16[2,128,512]{2,1,0:T(8,128)(2,1)S(1)} %get-tuple-element.33), channel_id=1, source_target_pairs={{0,3},{1,0},{2,1},{3,2},{8,104},{9,105},{10,106},{11,107},{4,7},{5... | collective-permute-start | bytes 786440 | tf_op jit(solution)/shard_map/ppermute | solution.py:30
  78.5 2.7 %collective-permute-start.13 = (bf16[2,128,512]{2,1,0:T(8,128)(2,1)S(1)}, bf16[2,128,512]{2,1,0:T(8,128)(2,1)S(1)}, u32[]{:S(2)}, u32[]{:S(2)}) collective-permute-start(bf16[2,128,512]{2,1,0:T(8,128)(2,1)S(1)} %get-tuple-element.36), channel_id=1, source_target_pairs={{0,3},{1,0},{2,1},{3,2},{8,104},{9,105},{10,106},{11,107},{4,7},{5... | collective-permute-start | bytes 786440 | tf_op jit(solution)/shard_map/ppermute | solution.py:30
  82.0 3.1 %collective-permute-start.10 = (bf16[2,128,512]{2,1,0:T(8,128)(2,1)S(1)}, bf16[2,128,512]{2,1,0:T(8,128)(2,1)S(1)}, u32[]{:S(2)}, u32[]{:S(2)}) collective-permute-start(bf16[2,128,512]{2,1,0:T(8,128)(2,1)S(1)} %add_convert_fusion.8), channel_id=1, source_target_pairs={{0,3},{1,0},{2,1},{3,2},{8,104},{9,105},{10,106},{11,107},{4,7},{5... | collective-permute-start | bytes 786440 | tf_op jit(solution)/shard_map/ppermute | solution.py:30
  85.3 2.7 %collective-permute-done.8 = bf16[2,128,512]{2,1,0:T(8,128)(2,1)S(1)} collective-permute-done((bf16[2,128,512]{2,1,0:T(8,128)(2,1)S(1)}, bf16[2,128,512]{2,1,0:T(8,128)(2,1)S(1)}, u32[]{:S(2)}, u32[]{:S(2)}) %collective-permute-start.8) | collective-permute-done | bytes 262176 | tf_op jit(solution)/shard_map/ppermute | solution.py:30
  88.4 3.5 %collective-permute-done.12 = bf16[2,128,512]{2,1,0:T(8,128)(2,1)S(1)} collective-permute-done((bf16[2,128,512]{2,1,0:T(8,128)(2,1)S(1)}, bf16[2,128,512]{2,1,0:T(8,128)(2,1)S(1)}, u32[]{:S(2)}, u32[]{:S(2)}) %collective-permute-start.12) | collective-permute-done | bytes 262176 | tf_op jit(solution)/shard_map/ppermute | solution.py:30
  92.3 1.7 %collective-permute-start.14 = (bf16[128,512]{1,0:T(8,128)(2,1)S(1)}, bf16[128,512]{1,0:T(8,128)(2,1)S(1)}, u32[]{:S(2)}, u32[]{:S(2)}) collective-permute-start(bf16[128,512]{1,0:T(8,128)(2,1)S(1)} %get-tuple-element.48), channel_id=1, source_target_pairs={{0,4},{1,5},{2,6},{3,7},{8,12},{9,13},{10,14},{11,15},{4,16},{5,17... | collective-permute-start | bytes 393224 | tf_op jit(solution)/shard_map/ppermute | solution.py:30
  94.0 2.2 %collective-permute-start.15 = (bf16[128,512]{1,0:T(8,128)(2,1)S(1)}, bf16[128,512]{1,0:T(8,128)(2,1)S(1)}, u32[]{:S(2)}, u32[]{:S(2)}) collective-permute-start(bf16[128,512]{1,0:T(8,128)(2,1)S(1)} %get-tuple-element.49), channel_id=1, source_target_pairs={{0,20},{1,21},{2,22},{3,23},{8,28},{9,29},{10,30},{11,31},{4,0},{5... | collective-permute-start | bytes 393224 | tf_op jit(solution)/shard_map/ppermute | solution.py:30
  98.5 3.0 %collective-permute-done.16 = bf16[128,512]{1,0:T(8,128)(2,1)S(1)} collective-permute-done((bf16[128,512]{1,0:T(8,128)(2,1)S(1)}, bf16[128,512]{1,0:T(8,128)(2,1)S(1)}, u32[]{:S(2)}, u32[]{:S(2)}) %collective-permute-start.16) | collective-permute-done | bytes 131104 | tf_op jit(solution)/shard_map/ppermute | solution.py:30
  102.7 6.5 %collective-permute-start.17 = (bf16[128,512]{1,0:T(8,128)(2,1)S(1)}, bf16[128,512]{1,0:T(8,128)(2,1)S(1)}, u32[]{:S(2)}, u32[]{:S(2)}) collective-permute-start(bf16[128,512]{1,0:T(8,128)(2,1)S(1)} %get-tuple-element.38), channel_id=1, source_target_pairs={{0,8},{1,9},{2,10},{3,11},{8,0},{9,1},{10,2},{11,3},{4,12},{5,13},... | collective-permute-start | bytes 393224 | tf_op jit(solution)/shard_map/ppermute | solution.py:30
  112.3 5.6 %collective-permute-done.18.refs_1_ = bf16[2,128,512]{2,1,0:T(8,128)(2,1)S(1)} collective-permute-done((bf16[2,128,512]{2,1,0:T(8,128)(2,1)S(1)}, bf16[2,128,512]{2,1,0:T(8,128)(2,1)S(1)}, u32[]{:S(2)}, u32[]{:S(2)}) %collective-permute-start.18) | collective-permute-done | bytes 262176 | tf_op jit(solution)/shard_map/ppermute | solution.py:30
  118.8 1.5 %collective-permute-start.21 = (bf16[128,512]{1,0:T(8,128)(2,1)S(1)}, bf16[128,512]{1,0:T(8,128)(2,1)S(1)}, u32[]{:S(2)}, u32[]{:S(2)}) collective-permute-start(bf16[128,512]{1,0:T(8,128)(2,1)S(1)} %get-tuple-element.38), channel_id=1, source_target_pairs={{0,16},{1,17},{2,18},{3,19},{8,24},{9,25},{10,26},{11,27},{4,20},{... | collective-permute-start | bytes 393224 | tf_op jit(solution)/shard_map/ppermute | solution.py:30
  120.3 2.0 %collective-permute-start.23 = (bf16[2,128,512]{2,1,0:T(8,128)(2,1)S(1)}, bf16[2,128,512]{2,1,0:T(8,128)(2,1)S(1)}, u32[]{:S(2)}, u32[]{:S(2)}) collective-permute-start(bf16[2,128,512]{2,1,0:T(8,128)(2,1)S(1)} %collective-permute-done.19.refs_2_), channel_id=1, source_target_pairs={{0,8},{1,9},{2,10},{3,11},{8,0},{9,1},{10,2},{11,3},{4,12},{5,13},... | collective-permute-start | bytes 786440 | tf_op jit(solution)/shard_map/ppermute | solution.py:30
  123.4 2.4 %collective-permute-start.24 = (bf16[2,128,512]{2,1,0:T(8,128)(2,1)S(1)}, bf16[2,128,512]{2,1,0:T(8,128)(2,1)S(1)}, u32[]{:S(2)}, u32[]{:S(2)}) collective-permute-start(bf16[2,128,512]{2,1,0:T(8,128)(2,1)S(1)} %collective-permute-done.20.refs_3_), channel_id=1, source_target_pairs={{0,8},{1,9},{2,10},{3,11},{8,0},{9,1},{10,2},{11,3},{4,12},{5,13},... | collective-permute-start | bytes 786440 | tf_op jit(solution)/shard_map/ppermute | solution.py:30
  (54 shorter events, 19.8 us)
Async XLA Ops:
  14.1 17.8 %collective-permute-start = (bf16[3,4,4,128,512]{4,3,2,1,0:T(8,128)(2,1)S(1)}, bf16[3,4,4,128,512]{4,3,2,1,0:T(8,128)(2,1)S(1)}, u32[]{:S(2)}, u32[]{:S(2)}) collective-permute-start(bf16[3,4,4,128,512]{4,3,2,1,0:T(8,128)(2,1)S(1)} %get-tuple-element.23), channel_id=1, source_target_pairs={{0,8},{1,9},{2,10},{3,11},{8,0},{9,1},{10,2},{11,3},{4,12},{5,13},... | collective-permute-start | bytes 18874376 | tf_op jit(solution)/shard_map/ppermute | solution.py:30
  15.6 12.8 %collective-permute-start.1 = (bf16[4,4,128,512]{3,2,1,0:T(8,128)(2,1)S(1)}, bf16[4,4,128,512]{3,2,1,0:T(8,128)(2,1)S(1)}, u32[]{:S(2)}, u32[]{:S(2)}) collective-permute-start(bf16[4,4,128,512]{3,2,1,0:T(8,128)(2,1)S(1)} %get-tuple-element.25), channel_id=1, source_target_pairs={{0,8},{1,9},{2,10},{3,11},{8,0},{9,1},{10,2},{11,3},{4,12},{5,13},... | collective-permute-start | bytes 6291464 | tf_op jit(solution)/shard_map/ppermute | solution.py:30
  29.1 14.7 %collective-permute-start.3 = (bf16[2,4,128,512]{3,2,1,0:T(8,128)(2,1)S(1)}, bf16[2,4,128,512]{3,2,1,0:T(8,128)(2,1)S(1)}, u32[]{:S(2)}, u32[]{:S(2)}) collective-permute-start(bf16[2,4,128,512]{3,2,1,0:T(8,128)(2,1)S(1)} %get-tuple-element.47), channel_id=1, source_target_pairs={{0,96},{1,97},{2,98},{3,99},{8,11},{9,8},{10,9},{11,10},{4,100},{5... | collective-permute-start | bytes 3145736 | tf_op jit(solution)/shard_map/ppermute | solution.py:30
  32.0 15.2 %collective-permute-start.5 = (bf16[2,4,128,512]{3,2,1,0:T(8,128)(2,1)S(1)}, bf16[2,4,128,512]{3,2,1,0:T(8,128)(2,1)S(1)}, u32[]{:S(2)}, u32[]{:S(2)}) collective-permute-start(bf16[2,4,128,512]{3,2,1,0:T(8,128)(2,1)S(1)} %get-tuple-element.46), channel_id=1, source_target_pairs={{0,32},{1,33},{2,34},{3,35},{8,9},{9,10},{10,11},{11,8},{4,36},{5,... | collective-permute-start | bytes 3145736 | tf_op jit(solution)/shard_map/ppermute | solution.py:30
  48.1 14.0 %collective-permute-start.4 = (bf16[2,4,128,512]{3,2,1,0:T(8,128)(2,1)S(1)}, bf16[2,4,128,512]{3,2,1,0:T(8,128)(2,1)S(1)}, u32[]{:S(2)}, u32[]{:S(2)}) collective-permute-start(bf16[2,4,128,512]{3,2,1,0:T(8,128)(2,1)S(1)} %get-tuple-element.43), channel_id=1, source_target_pairs={{0,96},{1,97},{2,98},{3,99},{8,11},{9,8},{10,9},{11,10},{4,100},{5... | collective-permute-start | bytes 3145736 | tf_op jit(solution)/shard_map/ppermute | solution.py:30
  48.2 15.2 %collective-permute-start.6 = (bf16[2,4,128,512]{3,2,1,0:T(8,128)(2,1)S(1)}, bf16[2,4,128,512]{3,2,1,0:T(8,128)(2,1)S(1)}, u32[]{:S(2)}, u32[]{:S(2)}) collective-permute-start(bf16[2,4,128,512]{3,2,1,0:T(8,128)(2,1)S(1)} %get-tuple-element.42), channel_id=1, source_target_pairs={{0,32},{1,33},{2,34},{3,35},{8,9},{9,10},{10,11},{11,8},{4,36},{5,... | collective-permute-start | bytes 3145736 | tf_op jit(solution)/shard_map/ppermute | solution.py:30
  49.6 25.0 %collective-permute-start.2 = (bf16[2,4,128,512]{3,2,1,0:T(8,128)(2,1)S(1)}, bf16[2,4,128,512]{3,2,1,0:T(8,128)(2,1)S(1)}, u32[]{:S(2)}, u32[]{:S(2)}) collective-permute-start(bf16[2,4,128,512]{3,2,1,0:T(8,128)(2,1)S(1)} %get-tuple-element.45), channel_id=1, source_target_pairs={{0,32},{1,33},{2,34},{3,35},{8,9},{9,10},{10,11},{11,8},{4,36},{5,... | collective-permute-start | bytes 3145736 | tf_op jit(solution)/shard_map/ppermute | solution.py:30
  49.7 25.0 %collective-permute-start.7 = (bf16[2,4,128,512]{3,2,1,0:T(8,128)(2,1)S(1)}, bf16[2,4,128,512]{3,2,1,0:T(8,128)(2,1)S(1)}, u32[]{:S(2)}, u32[]{:S(2)}) collective-permute-start(bf16[2,4,128,512]{3,2,1,0:T(8,128)(2,1)S(1)} %get-tuple-element.44), channel_id=1, source_target_pairs={{0,96},{1,97},{2,98},{3,99},{8,11},{9,8},{10,9},{11,10},{4,100},{5... | collective-permute-start | bytes 3145736 | tf_op jit(solution)/shard_map/ppermute | solution.py:30
  76.3 5.6 %collective-permute-start.9 = (bf16[2,128,512]{2,1,0:T(8,128)(2,1)S(1)}, bf16[2,128,512]{2,1,0:T(8,128)(2,1)S(1)}, u32[]{:S(2)}, u32[]{:S(2)}) collective-permute-start(bf16[2,128,512]{2,1,0:T(8,128)(2,1)S(1)} %get-tuple-element.33), channel_id=1, source_target_pairs={{0,3},{1,0},{2,1},{3,2},{8,104},{9,105},{10,106},{11,107},{4,7},{5... | collective-permute-start | bytes 786440 | tf_op jit(solution)/shard_map/ppermute | solution.py:30
  78.5 6.6 %collective-permute-start.11 = (bf16[2,128,512]{2,1,0:T(8,128)(2,1)S(1)}, bf16[2,128,512]{2,1,0:T(8,128)(2,1)S(1)}, u32[]{:S(2)}, u32[]{:S(2)}) collective-permute-start(bf16[2,128,512]{2,1,0:T(8,128)(2,1)S(1)} %get-tuple-element.35), channel_id=1, source_target_pairs={{0,1},{1,2},{2,3},{3,0},{8,40},{9,41},{10,42},{11,43},{4,5},{5,6},... | collective-permute-start | bytes 786440 | tf_op jit(solution)/shard_map/ppermute | solution.py:30
  78.5 6.9 %collective-permute-start.13 = (bf16[2,128,512]{2,1,0:T(8,128)(2,1)S(1)}, bf16[2,128,512]{2,1,0:T(8,128)(2,1)S(1)}, u32[]{:S(2)}, u32[]{:S(2)}) collective-permute-start(bf16[2,128,512]{2,1,0:T(8,128)(2,1)S(1)} %get-tuple-element.36), channel_id=1, source_target_pairs={{0,3},{1,0},{2,1},{3,2},{8,104},{9,105},{10,106},{11,107},{4,7},{5... | collective-permute-start | bytes 786440 | tf_op jit(solution)/shard_map/ppermute | solution.py:30
  81.1 6.9 %collective-permute-start.8 = (bf16[2,128,512]{2,1,0:T(8,128)(2,1)S(1)}, bf16[2,128,512]{2,1,0:T(8,128)(2,1)S(1)}, u32[]{:S(2)}, u32[]{:S(2)}) collective-permute-start(bf16[2,128,512]{2,1,0:T(8,128)(2,1)S(1)} %get-tuple-element.31), channel_id=1, source_target_pairs={{0,1},{1,2},{2,3},{3,0},{8,40},{9,41},{10,42},{11,43},{4,5},{5,6},... | collective-permute-start | bytes 786440 | tf_op jit(solution)/shard_map/ppermute | solution.py:30
  82.0 6.4 %collective-permute-start.10 = (bf16[2,128,512]{2,1,0:T(8,128)(2,1)S(1)}, bf16[2,128,512]{2,1,0:T(8,128)(2,1)S(1)}, u32[]{:S(2)}, u32[]{:S(2)}) collective-permute-start(bf16[2,128,512]{2,1,0:T(8,128)(2,1)S(1)} %add_convert_fusion.8), channel_id=1, source_target_pairs={{0,3},{1,0},{2,1},{3,2},{8,104},{9,105},{10,106},{11,107},{4,7},{5... | collective-permute-start | bytes 786440 | tf_op jit(solution)/shard_map/ppermute | solution.py:30
  85.1 6.8 %collective-permute-start.12 = (bf16[2,128,512]{2,1,0:T(8,128)(2,1)S(1)}, bf16[2,128,512]{2,1,0:T(8,128)(2,1)S(1)}, u32[]{:S(2)}, u32[]{:S(2)}) collective-permute-start(bf16[2,128,512]{2,1,0:T(8,128)(2,1)S(1)} %add_convert_fusion.6), channel_id=1, source_target_pairs={{0,1},{1,2},{2,3},{3,0},{8,40},{9,41},{10,42},{11,43},{4,5},{5,6},... | collective-permute-start | bytes 786440 | tf_op jit(solution)/shard_map/ppermute | solution.py:30
  92.3 6.2 %collective-permute-start.14 = (bf16[128,512]{1,0:T(8,128)(2,1)S(1)}, bf16[128,512]{1,0:T(8,128)(2,1)S(1)}, u32[]{:S(2)}, u32[]{:S(2)}) collective-permute-start(bf16[128,512]{1,0:T(8,128)(2,1)S(1)} %get-tuple-element.48), channel_id=1, source_target_pairs={{0,4},{1,5},{2,6},{3,7},{8,12},{9,13},{10,14},{11,15},{4,16},{5,17... | collective-permute-start | bytes 393224 | tf_op jit(solution)/shard_map/ppermute | solution.py:30
  94.0 4.5 %collective-permute-start.15 = (bf16[128,512]{1,0:T(8,128)(2,1)S(1)}, bf16[128,512]{1,0:T(8,128)(2,1)S(1)}, u32[]{:S(2)}, u32[]{:S(2)}) collective-permute-start(bf16[128,512]{1,0:T(8,128)(2,1)S(1)} %get-tuple-element.49), channel_id=1, source_target_pairs={{0,20},{1,21},{2,22},{3,23},{8,28},{9,29},{10,30},{11,31},{4,0},{5... | collective-permute-start | bytes 393224 | tf_op jit(solution)/shard_map/ppermute | solution.py:30
  96.2 5.3 %collective-permute-start.16 = (bf16[128,512]{1,0:T(8,128)(2,1)S(1)}, bf16[128,512]{1,0:T(8,128)(2,1)S(1)}, u32[]{:S(2)}, u32[]{:S(2)}) collective-permute-start(bf16[128,512]{1,0:T(8,128)(2,1)S(1)} %get-tuple-element.50), channel_id=1, source_target_pairs={{0,16},{1,17},{2,18},{3,19},{8,24},{9,25},{10,26},{11,27},{4,20},{... | collective-permute-start | bytes 393224 | tf_op jit(solution)/shard_map/ppermute | solution.py:30
  102.7 7.5 %collective-permute-start.17 = (bf16[128,512]{1,0:T(8,128)(2,1)S(1)}, bf16[128,512]{1,0:T(8,128)(2,1)S(1)}, u32[]{:S(2)}, u32[]{:S(2)}) collective-permute-start(bf16[128,512]{1,0:T(8,128)(2,1)S(1)} %get-tuple-element.38), channel_id=1, source_target_pairs={{0,8},{1,9},{2,10},{3,11},{8,0},{9,1},{10,2},{11,3},{4,12},{5,13},... | collective-permute-start | bytes 393224 | tf_op jit(solution)/shard_map/ppermute | solution.py:30
  110.2 7.7 %collective-permute-start.18 = (bf16[2,128,512]{2,1,0:T(8,128)(2,1)S(1)}, bf16[2,128,512]{2,1,0:T(8,128)(2,1)S(1)}, u32[]{:S(2)}, u32[]{:S(2)}) collective-permute-start(bf16[2,128,512]{2,1,0:T(8,128)(2,1)S(1)} %pad_maximum_fusion.refs_0_), channel_id=1, source_target_pairs={{0,32},{1,33},{2,34},{3,35},{8,120},{9,121},{10,122},{11,123},{4,3... | collective-permute-start | bytes 786440 | tf_op jit(solution)/shard_map/ppermute | solution.py:30
  111.1 9.1 %collective-permute-start.19 = (bf16[2,128,512]{2,1,0:T(8,128)(2,1)S(1)}, bf16[2,128,512]{2,1,0:T(8,128)(2,1)S(1)}, u32[]{:S(2)}, u32[]{:S(2)}) collective-permute-start(bf16[2,128,512]{2,1,0:T(8,128)(2,1)S(1)} %pad_maximum_fusion.refs_0_), channel_id=1, source_target_pairs={{0,48},{1,49},{2,50},{3,51},{8,104},{9,105},{10,106},{11,107},{4,5... | collective-permute-start | bytes 786440 | tf_op jit(solution)/shard_map/ppermute | solution.py:30
  117.9 5.5 %collective-permute-start.20 = (bf16[2,128,512]{2,1,0:T(8,128)(2,1)S(1)}, bf16[2,128,512]{2,1,0:T(8,128)(2,1)S(1)}, u32[]{:S(2)}, u32[]{:S(2)}) collective-permute-start(bf16[2,128,512]{2,1,0:T(8,128)(2,1)S(1)} %collective-permute-done.18.refs_1_), channel_id=1, source_target_pairs={{0,32},{1,33},{2,34},{3,35},{8,104},{9,105},{10,106},{11,107},{4,3... | collective-permute-start | bytes 786440 | tf_op jit(solution)/shard_map/ppermute | solution.py:30
  118.8 7.1 %collective-permute-start.21 = (bf16[128,512]{1,0:T(8,128)(2,1)S(1)}, bf16[128,512]{1,0:T(8,128)(2,1)S(1)}, u32[]{:S(2)}, u32[]{:S(2)}) collective-permute-start(bf16[128,512]{1,0:T(8,128)(2,1)S(1)} %get-tuple-element.38), channel_id=1, source_target_pairs={{0,16},{1,17},{2,18},{3,19},{8,24},{9,25},{10,26},{11,27},{4,20},{... | collective-permute-start | bytes 393224 | tf_op jit(solution)/shard_map/ppermute | solution.py:30
  120.3 6.9 %collective-permute-start.22 = (bf16[2,128,512]{2,1,0:T(8,128)(2,1)S(1)}, bf16[2,128,512]{2,1,0:T(8,128)(2,1)S(1)}, u32[]{:S(2)}, u32[]{:S(2)}) collective-permute-start(bf16[2,128,512]{2,1,0:T(8,128)(2,1)S(1)} %collective-permute-done.18.refs_1_), channel_id=1, source_target_pairs={{0,8},{1,9},{2,10},{3,11},{8,0},{9,1},{10,2},{11,3},{4,12},{5,13},... | collective-permute-start | bytes 786440 | tf_op jit(solution)/shard_map/ppermute | solution.py:30
  120.3 6.9 %collective-permute-start.23 = (bf16[2,128,512]{2,1,0:T(8,128)(2,1)S(1)}, bf16[2,128,512]{2,1,0:T(8,128)(2,1)S(1)}, u32[]{:S(2)}, u32[]{:S(2)}) collective-permute-start(bf16[2,128,512]{2,1,0:T(8,128)(2,1)S(1)} %collective-permute-done.19.refs_2_), channel_id=1, source_target_pairs={{0,8},{1,9},{2,10},{3,11},{8,0},{9,1},{10,2},{11,3},{4,12},{5,13},... | collective-permute-start | bytes 786440 | tf_op jit(solution)/shard_map/ppermute | solution.py:30
  (7 other events, 67.2 us)
